TPU v7x, 128 devices: a whole 4x4x4 slice. The times are simulated.
128 devices in a mesh: lat: 2 (over x_lo), lon: 8 (over z_lo, x_hi, core), lev: 8 (over z_hi, y).
Axes of the slice: x: 4 (x_hi: 2, x_lo: 2; x = x_hi * 2 + x_lo), y: 4, z: 4 (z_hi: 2, z_lo: 2; z = z_hi * 2 + z_lo), core: 2. Of those that a mesh axis runs over, the one named last changes fastest.
Arguments:
- initial_state: float32 [16, 256, 512, 128], P('lat', 'lon', 'lev'), may hold values from 0.2 to 1.8
- scaled_diffusivity: float32 [16, 256, 512, 128], P('lat', 'lon', 'lev'), may hold values from 0.03 to 0.15
- scaled_forcing: float32 [16, 256, 512, 128], P('lat', 'lon', 'lev'), may hold values from -0.2 to 0.2
Outputs:
- cumulative_totals: float32 [16, 256, 512, 128], P('lat', 'lon', 'lev')
- temperature_end: float32 [16, 256, 512, 128], P('lat', 'lon', 'lev')
All inputs are finite; a program needn't handle non-finite values.
Results may differ from a plain program's by a relative error of at most 0.00002.
Values sent between devices are 32-bit elements; how exact they have to be, the bound alone decides.
A program may use at most 128 MiB of HBM per device.

v0:
```python
import functools

import jax
import jax.numpy as jnp
from jax import lax
from jax.experimental import pallas as pl
from jax.experimental.pallas import tpu as pltpu
from jax.sharding import PartitionSpec as P

STEPS = 4
PAD = 8
CHUNK = 8
MESH = pl.DeviceIdType.MESH


def steps_kernel(
    sizes, x, d, f, end, before, state, coef, source,
    lev_out, lev_in, tot_mid, tot_edge, mid_in, edge_in,
    lat_send, lat_recv, lon_send, lon_recv, lev_send, lev_recv,
    load_sem, tot_send, tot_recv,
):
    J, I, K, M = x.shape
    chunks = K // CHUNK
    me = {axis: lax.axis_index(axis) for axis in sizes}
    n_lon = sizes["lon"]
    rows = pl.ds(1, I)
    levels = pl.ds(PAD, K)
    planes = pl.ds(1, J)

    def has(axis, side):
        return me[axis] > 0 if side == 0 else me[axis] < sizes[axis] - 1

    def beside(axis, side):
        return {axis: me[axis] - 1 if side == 0 else me[axis] + 1}

    def both(axis, act):
        if sizes[axis] > 1:
            for side in (0, 1):
                pl.when(has(axis, side))(functools.partial(act, side))

    def load(which, j):
        src, dst = (
            (x.at[j], state.at[0, j + 1, rows, levels]),
            (d.at[j], coef.at[j]),
            (f.at[j], source.at[j]),
        )[which]
        return pltpu.make_async_copy(src, dst, load_sem.at[which, j])

    for which in range(3):
        for j in range(J):
            load(which, j).start()

    barrier = pltpu.get_barrier_semaphore()
    count = jnp.int32(n_lon - 1)

    def greet(target):
        pl.semaphore_signal(barrier, inc=1, device_id=target, device_id_type=MESH)

    for axis in ("lat", "lev"):
        both(axis, lambda side, axis=axis: greet(beside(axis, side)))
        if sizes[axis] > 1:
            count = count + has(axis, 0).astype(jnp.int32) + has(axis, 1).astype(jnp.int32)
    for other in range(n_lon):
        pl.when(other != me["lon"])(lambda other=other: greet({"lon": jnp.int32(other)}))
    pl.semaphore_wait(barrier, count)

    def lat_copy(step, side, c):
        slot = step % 2
        part = pl.ds(pl.multiple_of(PAD + c * CHUNK, CHUNK), CHUNK)
        plane, target = (1, J + 1) if side == 0 else (J, 0)
        if step == 0:
            inner = pl.ds(pl.multiple_of(c * CHUNK, CHUNK), CHUNK)
            src = x.at[plane - 1, :, inner]
        else:
            src = state.at[slot, plane, rows, part]
        return pltpu.make_async_remote_copy(
            src_ref=src,
            dst_ref=state.at[slot, target, rows, part],
            send_sem=lat_send.at[slot, side, c],
            recv_sem=lat_recv.at[slot, 1 - side, c],
            device_id=beside("lat", side),
            device_id_type=MESH,
        )

    def lat_arrived(step, side, c):
        slot = step % 2
        part = pl.ds(pl.multiple_of(PAD + c * CHUNK, CHUNK), CHUNK)
        target = 0 if side == 0 else J + 1
        pltpu.make_async_remote_copy(
            src_ref=state.at[slot, target, rows, part],
            dst_ref=state.at[slot, target, rows, part],
            send_sem=lat_send.at[slot, side, c],
            recv_sem=lat_recv.at[slot, side, c],
            device_id=beside("lat", side),
            device_id_type=MESH,
        ).wait_recv()

    def lon_copy(step, side, arriving=False):
        slot = step % 2
        row, target = (1, I + 1) if side == 0 else (I, 0)
        dst = (0 if side == 0 else I + 1) if arriving else target
        return pltpu.make_async_remote_copy(
            src_ref=state.at[slot, planes, row, levels],
            dst_ref=state.at[slot, planes, dst, levels],
            send_sem=lon_send.at[slot, side],
            recv_sem=lon_recv.at[slot, side if arriving else 1 - side],
            device_id=beside("lon", side),
            device_id_type=MESH,
        )

    def lev_copy(step, side, arriving=False):
        slot = step % 2
        landing = side if arriving else 1 - side
        return pltpu.make_async_remote_copy(
            src_ref=lev_out.at[side],
            dst_ref=lev_in.at[slot, landing],
            send_sem=lev_send.at[slot, side],
            recv_sem=lev_recv.at[slot, landing],
            device_id=beside("lev", side),
            device_id_type=MESH,
        )

    def lat_start(step, c):
        both("lat", lambda side: lat_copy(step, side, c).start())

    for c in range(chunks):
        lat_start(0, c)

    def clear(axis, side):
        for slot in (0, 1):
            if axis == "lat":
                target = 0 if side == 0 else J + 1

                @pl.loop(1, I + 1)
                def _(i):
                    state[slot, target, i, PAD : PAD + K, :] = jnp.zeros((K, M), jnp.float32)
            elif axis == "lon":
                target = 0 if side == 0 else I + 1
                for p in range(1, J + 1):
                    state[slot, p, target, PAD : PAD + K, :] = jnp.zeros((K, M), jnp.float32)
            else:
                target = PAD - 1 if side == 0 else PAD + K

                @pl.loop(1, J + 1)
                def _(p):
                    state[slot, p, 1 : I + 1, target : target + 1, :] = jnp.zeros(
                        (I, 1, M), jnp.float32
                    )

    for axis in ("lat", "lon", "lev"):
        for side in (0, 1):
            pl.when(jnp.logical_not(has(axis, side)))(functools.partial(clear, axis, side))

    for j in range(J):
        load(0, j).wait()

    def update(step, p, i, start, length):
        a, b = step % 2, (step + 1) % 2
        here = pl.ds(start, length)
        inner = pl.ds(start - PAD, length)
        middle = state[a, p, i, here, :]
        spread = (
            (state[a, p - 1, i, here, :] + state[a, p + 1, i, here, :])
            + (state[a, p, i - 1, here, :] + state[a, p, i + 1, here, :])
            + (
                state[a, p, i, pl.ds(start - 1, length), :]
                + state[a, p, i, pl.ds(start + 1, length), :]
            )
            - 6.0 * middle
        )
        new = middle + coef[p - 1, i - 1, inner, :] * spread + source[p - 1, i - 1, inner, :]
        if step == STEPS - 1:
            end[p - 1, i - 1, inner, :] = new
        else:
            state[b, p, i, here, :] = new
        return new

    def mid_total(target, arriving=None):
        sender = me["lon"] if arriving is None else arriving
        return pltpu.make_async_remote_copy(
            src_ref=tot_mid,
            dst_ref=mid_in.at[sender],
            send_sem=tot_send.at[target, chunks],
            recv_sem=tot_recv.at[sender, chunks],
            device_id={"lon": jnp.int32(target)},
            device_id_type=MESH,
        )

    def edge_total(target, c, arriving=None):
        sender = me["lon"] if arriving is None else arriving
        part = pl.ds(pl.multiple_of(c * CHUNK, CHUNK), CHUNK)
        return pltpu.make_async_remote_copy(
            src_ref=tot_edge.at[:, part],
            dst_ref=edge_in.at[sender, :, part],
            send_sem=tot_send.at[target, c],
            recv_sem=tot_recv.at[sender, c],
            device_id={"lon": jnp.int32(target)},
            device_id_type=MESH,
        )

    def later(act):
        for other in range(1, n_lon):
            pl.when(other > me["lon"])(functools.partial(act, other))

    def earlier(act):
        for other in range(n_lon - 1):
            pl.when(other < me["lon"])(functools.partial(act, other))

    for step in range(STEPS):
        a, b = step % 2, (step + 1) % 2
        last = step == STEPS - 1

        both("lon", lambda side: lon_copy(step, side).start())
        if sizes["lev"] > 1:

            @pl.loop(1, J + 1)
            def _(p):
                lev_out[0, p - 1] = state[a, p, 1 : I + 1, PAD : PAD + 1, :]
                lev_out[1, p - 1] = state[a, p, 1 : I + 1, PAD + K - 1 : PAD + K, :]

        both("lev", lambda side: lev_copy(step, side).start())
        if step == 0:
            for j in range(J):
                load(1, j).wait()
                load(2, j).wait()

        def lon_done(side):
            lon_copy(step, side).wait_send()
            lon_copy(step, side, True).wait_recv()

        def lev_done(side):
            lev_copy(step, side).wait_send()
            lev_copy(step, side, True).wait_recv()
            row = PAD - 1 if side == 0 else PAD + K

            @pl.loop(1, J + 1)
            def _(p):
                state[a, p, 1 : I + 1, row : row + 1, :] = lev_in[a, side, p - 1]

        both("lon", lon_done)
        both("lev", lev_done)

        @pl.loop(2, J)
        def _(p):
            if last:
                tot_mid[p - 2] = lax.fori_loop(
                    1,
                    I + 1,
                    lambda i, total: total + update(step, p, i, PAD, K),
                    jnp.zeros((K, M), jnp.float32),
                )
            else:

                @pl.loop(1, I + 1)
                def _(i):
                    update(step, p, i, PAD, K)

        if last:
            later(lambda other: mid_total(other).start())

        @pl.loop(0, chunks)
        def _(c):
            def ready(side):
                if step > 0:
                    lat_copy(step - 1, side, c).wait_send()
                lat_arrived(step, side, c)

            both("lat", ready)
            start = pl.multiple_of(PAD + c * CHUNK, CHUNK)
            zero = jnp.zeros((CHUNK, M), jnp.float32)

            def row(i, totals):
                return (
                    totals[0] + update(step, 1, i, start, CHUNK),
                    totals[1] + update(step, J, i, start, CHUNK),
                )

            low, high = lax.fori_loop(1, I + 1, row, (zero, zero), unroll=4)
            if last:
                part = pl.ds(pl.multiple_of(c * CHUNK, CHUNK), CHUNK)
                tot_edge[0, part, :] = low
                tot_edge[1, part, :] = high
                later(lambda other: edge_total(other, c).start())
            else:
                lat_start(step + 1, c)

    before[...] = jnp.zeros(before.shape, jnp.float32)

    def add_mid(other):
        mid_total(other, other).wait_recv()
        before[1 : J - 1] += mid_in[other]

    def add_edge(other):
        for c in range(chunks):
            edge_total(other, c, other).wait_recv()
        before[0] += edge_in[other, 0]
        before[J - 1] += edge_in[other, 1]

    earlier(add_mid)
    earlier(add_edge)

    for c in range(chunks):
        both("lat", lambda side: lat_copy(STEPS - 1, side, c).wait_send())
        later(lambda other: edge_total(other, c).wait_send())
    later(lambda other: mid_total(other).wait_send())


def totals_kernel(scale, x, before, totals, end, sums, end_sem, sums_sem):
    J, I = x.shape[:2]

    def out(which, j):
        src, dst, sem = ((x, end, end_sem), (sums, totals, sums_sem))[which]
        return pltpu.make_async_copy(src.at[j], dst.at[j], sem.at[j])

    for j in range(J):
        out(0, j).start()

    @pl.loop(0, J)
    def _(j):
        def row(i, total):
            total = total + x[j, i]
            sums[j, i] = total * scale
            return total

        lax.fori_loop(0, I, row, before[j], unroll=4)
        out(1, j).start()

    for j in range(J):
        out(0, j).wait()
        out(1, j).wait()


def per_device(sizes, initial_state, scaled_diffusivity, scaled_forcing):
    J, I, K, M = initial_state.shape
    chunks = K // CHUNK
    n_lon = sizes["lon"]
    f32 = jnp.float32
    vmem = lambda *shape: pltpu.VMEM(shape, f32)
    sem = lambda *shape: pltpu.SemaphoreType.DMA(shape)
    hbm = pl.BlockSpec(memory_space=pltpu.HBM)
    local = pl.BlockSpec(memory_space=pltpu.VMEM)
    end, before = pl.pallas_call(
        functools.partial(steps_kernel, sizes),
        out_shape=(vmem(J, I, K, M), vmem(J, K, M)),
        in_specs=[hbm] * 3,
        out_specs=(local, local),
        scratch_shapes=[
            vmem(2, J + 2, I + 2, K + 2 * PAD, M),
            vmem(J, I, K, M),
            vmem(J, I, K, M),
            vmem(2, J, I, 1, M),
            vmem(2, 2, J, I, 1, M),
            vmem(J - 2, K, M),
            vmem(2, K, M),
            vmem(n_lon, J - 2, K, M),
            vmem(n_lon, 2, K, M),
            sem(2, 2, chunks),
            sem(2, 2, chunks),
            sem(2, 2),
            sem(2, 2),
            sem(2, 2),
            sem(2, 2),
            sem(3, J),
            sem(n_lon, chunks + 1),
            sem(n_lon, chunks + 1),
        ],
        compiler_params=pltpu.CompilerParams(
            collective_id=0, has_side_effects=True, vmem_limit_bytes=48 * 2**20
        ),
        name="steps",
    )(initial_state, scaled_diffusivity, scaled_forcing)

    return pl.pallas_call(
        functools.partial(totals_kernel, 1.0 / (I * n_lon)),
        out_shape=(jax.ShapeDtypeStruct((J, I, K, M), f32),) * 2,
        in_specs=[local, local],
        out_specs=(hbm, hbm),
        scratch_shapes=[vmem(J, I, K, M), sem(J), sem(J)],
        compiler_params=pltpu.CompilerParams(vmem_limit_bytes=20 * 2**20),
        name="totals",
    )(end, before)


def solution(mesh):
    spec = P("lat", "lon", "lev", None)
    return jax.shard_map(
        functools.partial(per_device, dict(mesh.shape)),
        mesh=mesh,
        in_specs=(spec,) * 3,
        out_specs=(spec,) * 2,
        check_vma=False,
    )
```

profile of v0, /device:TPU:57, one launch (start us, length us, event | category | flops | bytes accessed | tf_op | source)
XLA Modules:
  0.0 168.6 jit_solution(11400725473778501079)
XLA Ops:
  0.6 162.0 %steps.1 = (f32[8,32,64,128]{3,2,1,0:T(8,128)S(1)}, f32[8,64,128]{2,1,0:T(8,128)S(1)}) custom-call(f32[8,32,64,128]{3,2,1,0:T(8,128)} %x.1, f32[8,32,64,128]{3,2,1,0:T(8,128)} %d.1, f32[8,32,64,128]{3,2,1,0:T(8,128)} %f.1), custom_call_target="tpu_custom_call" | custom-call | tf_op jit(solution)/shard_map/steps/pallas_call | solution.py:342
  162.6 6.0 %totals.1 = (f32[8,32,64,128]{3,2,1,0:T(8,128)}, f32[8,32,64,128]{3,2,1,0:T(8,128)}) custom-call(f32[8,32,64,128]{3,2,1,0:T(8,128)S(1)} %get-tuple-element.4.x, f32[8,64,128]{2,1,0:T(8,128)S(1)} %get-tuple-element.5.before), custom_call_target="tpu_custom_call" | custom-call | tf_op jit(solution)/shard_map/totals/pallas_call | solution.py:373
where the time goes:
time: 170 us; the launch traced here: 169 us
  Pallas kernels  168 us (99%)
    pallas_call x1, Pallas kernels, per_device(): pl.pallas_call(functools.partial(steps_kernel, sizes), out_shape=(vmem(J,...  162 us
    pallas_call x1, Pallas kernels, per_device(): pl.pallas_call(functools.partial(totals_kernel, 1.0 / (I * n_lon)), out_s...  5.96 us

commit v1 on v0

v1 whole, which is shorter than its diff:
```python
import functools

import jax
import jax.numpy as jnp
from jax import lax
from jax.experimental import pallas as pl
from jax.experimental.pallas import tpu as pltpu
from jax.sharding import PartitionSpec as P

STEPS = 4
PAD = 8
CHUNK = 8
CORES = 2
MESH = pl.DeviceIdType.MESH


def steps_kernel(
    sizes, x, d, f, end, before, even, odd, coef, source,
    lev_out, lev_in, total, mate, chip, chip_in,
    lat_send, lat_recv, lon_send, lon_recv, lev_send, lev_recv,
    load_sem, mate_send, mate_recv, chip_send, chip_recv,
):
    J, I, K, M = x.shape
    chunks = K // CHUNK
    states = (even, odd)
    me = {axis: lax.axis_index(axis) for axis in sizes}
    n_lon = sizes["lon"]
    n_chips = n_lon // CORES
    my_chip = me["lon"] // CORES
    my_core = me["lon"] % CORES
    rows = pl.ds(1, I)
    levels = pl.ds(PAD, K)
    planes = pl.ds(1, J)

    def has(axis, side):
        return me[axis] > 0 if side == 0 else me[axis] < sizes[axis] - 1

    def beside(axis, side):
        return {axis: me[axis] - 1 if side == 0 else me[axis] + 1}

    def both(axis, act):
        if sizes[axis] > 1:
            for side in (0, 1):
                pl.when(has(axis, side))(functools.partial(act, side))

    def load(which, j):
        src, dst = (
            (x.at[j], even.at[j + 1, rows, levels]),
            (d.at[j], coef.at[j]),
            (f.at[j], source.at[j]),
        )[which]
        return pltpu.make_async_copy(src, dst, load_sem.at[which, j])

    for which in range(3):
        for j in range(J):
            load(which, j).start()

    barrier = pltpu.get_barrier_semaphore()
    count = jnp.int32(n_lon - 1)

    def greet(target):
        pl.semaphore_signal(barrier, inc=1, device_id=target, device_id_type=MESH)

    for axis in ("lat", "lev"):
        both(axis, lambda side, axis=axis: greet(beside(axis, side)))
        if sizes[axis] > 1:
            count = count + has(axis, 0).astype(jnp.int32) + has(axis, 1).astype(jnp.int32)
    for other in range(n_lon):
        pl.when(other != me["lon"])(lambda other=other: greet({"lon": jnp.int32(other)}))
    pl.semaphore_wait(barrier, count)

    def inside(c):
        return pl.ds(pl.multiple_of(c * CHUNK, CHUNK), CHUNK)

    def padded(c):
        return pl.ds(pl.multiple_of(PAD + c * CHUNK, CHUNK), CHUNK)

    def lat_copy(step, side, c, arriving=False):
        slot = step % 2
        state = states[slot]
        plane, target = (1, J + 1) if side == 0 else (J, 0)
        if arriving:
            target = 0 if side == 0 else J + 1
        if step == 0:
            src = x.at[plane - 1, :, inside(c)]
        else:
            src = state.at[plane, rows, padded(c)]
        return pltpu.make_async_remote_copy(
            src_ref=src,
            dst_ref=state.at[target, rows, padded(c)],
            send_sem=lat_send.at[slot, side, c],
            recv_sem=lat_recv.at[slot, side if arriving else 1 - side, c],
            device_id=beside("lat", side),
            device_id_type=MESH,
        )

    def lon_copy(step, side, c, arriving=False):
        slot = step % 2
        state = states[slot]
        row, target = (1, I + 1) if side == 0 else (I, 0)
        if arriving:
            target = 0 if side == 0 else I + 1
        if step == 0:
            src = x.at[:, row - 1, inside(c)]
        else:
            src = state.at[planes, row, padded(c)]
        return pltpu.make_async_remote_copy(
            src_ref=src,
            dst_ref=state.at[planes, target, padded(c)],
            send_sem=lon_send.at[slot, side, c],
            recv_sem=lon_recv.at[slot, side if arriving else 1 - side, c],
            device_id=beside("lon", side),
            device_id_type=MESH,
        )

    def lev_copy(step, side, arriving=False):
        slot = step % 2
        landing = side if arriving else 1 - side
        return pltpu.make_async_remote_copy(
            src_ref=lev_out.at[slot, side],
            dst_ref=lev_in.at[slot, landing],
            send_sem=lev_send.at[slot, side],
            recv_sem=lev_recv.at[slot, landing],
            device_id=beside("lev", side),
            device_id_type=MESH,
        )

    def send_chunk(step, c):
        both("lon", lambda side: lon_copy(step, side, c).start())
        both("lat", lambda side: lat_copy(step, side, c).start())

    def sent_chunk(step, c):
        both("lon", lambda side: lon_copy(step, side, c).wait_send())
        both("lat", lambda side: lat_copy(step, side, c).wait_send())

    def send_lev(step, side):
        state = states[step % 2]
        row = PAD if side == 0 else PAD + K - 1

        @pl.loop(1, J + 1)
        def _(p):
            lev_out[step % 2, side, p - 1] = state[p, 1 : I + 1, row : row + 1, :]

        lev_copy(step, side).start()

    def take_lev(step, side):
        state = states[step % 2]
        row = PAD - 1 if side == 0 else PAD + K
        lev_copy(step, side, True).wait_recv()

        @pl.loop(1, J + 1)
        def _(p):
            state[p, 1 : I + 1, row : row + 1, :] = lev_in[step % 2, side, p - 1]

    @pl.loop(0, chunks)
    def _(c):
        send_chunk(0, c)

    def clear(axis, side):
        for state in states:
            if axis == "lat":
                target = 0 if side == 0 else J + 1

                @pl.loop(1, I + 1)
                def _(i):
                    state[target, i, PAD : PAD + K, :] = jnp.zeros((K, M), jnp.float32)
            elif axis == "lon":
                target = 0 if side == 0 else I + 1
                for p in range(1, J + 1):
                    state[p, target, PAD : PAD + K, :] = jnp.zeros((K, M), jnp.float32)
            else:
                target = PAD - 1 if side == 0 else PAD + K

                @pl.loop(1, J + 1)
                def _(p):
                    state[p, 1 : I + 1, target : target + 1, :] = jnp.zeros(
                        (I, 1, M), jnp.float32
                    )

    for axis in ("lat", "lon", "lev"):
        for side in (0, 1):
            pl.when(jnp.logical_not(has(axis, side)))(functools.partial(clear, axis, side))

    for j in range(J):
        load(0, j).wait()
    both("lev", lambda side: send_lev(0, side))
    for j in range(J):
        load(1, j).wait()
        load(2, j).wait()

    def update(step, c):
        now, later = states[step % 2], states[(step + 1) % 2]
        last = step == STEPS - 1
        start = pl.multiple_of(PAD + c * CHUNK, CHUNK)
        here = pl.ds(start, CHUNK)
        inner = inside(c)

        def row(i, carry):
            past, mid, sums = carry
            coming = tuple(now[p, i + 1, here, :] for p in range(1, J + 1))
            column = (now[0, i, here, :],) + mid + (now[J + 1, i, here, :],)
            out = []
            for p in range(1, J + 1):
                spread = (
                    (column[p - 1] + column[p + 1])
                    + (past[p - 1] + coming[p - 1])
                    + (
                        now[p, i, pl.ds(start - 1, CHUNK), :]
                        + now[p, i, pl.ds(start + 1, CHUNK), :]
                    )
                    - 6.0 * column[p]
                )
                new = (
                    column[p]
                    + coef[p - 1, i - 1, inner, :] * spread
                    + source[p - 1, i - 1, inner, :]
                )
                if last:
                    end[p - 1, i - 1, inner, :] = new
                else:
                    later[p, i, here, :] = new
                out.append(new)
            if last:
                sums = tuple(total + new for total, new in zip(sums, out))
            return mid, coming, sums

        zero = jnp.zeros((CHUNK, M), jnp.float32)
        _, _, sums = lax.fori_loop(
            1,
            I + 1,
            row,
            (
                tuple(now[p, 0, here, :] for p in range(1, J + 1)),
                tuple(now[p, 1, here, :] for p in range(1, J + 1)),
                (zero,) * J if last else (),
            ),
            unroll=2,
        )
        return sums

    def mate_copy(c):
        return pltpu.make_async_remote_copy(
            src_ref=total.at[:, inside(c)],
            dst_ref=mate.at[:, inside(c)],
            send_sem=mate_send.at[c],
            recv_sem=mate_recv.at[c],
            device_id={"lon": me["lon"] + 1 - 2 * my_core},
            device_id_type=MESH,
        )

    def chip_copy(target, c, arriving=None):
        sender = my_chip if arriving is None else arriving
        return pltpu.make_async_remote_copy(
            src_ref=chip.at[:, inside(c)],
            dst_ref=chip_in.at[sender, :, inside(c)],
            send_sem=chip_send.at[target, c],
            recv_sem=chip_recv.at[sender, c],
            device_id={"lon": target * CORES + my_core},
            device_id_type=MESH,
        )

    def later_chips(act):
        for other in range(1, n_chips):
            pl.when(other > my_chip)(functools.partial(act, other))

    def earlier_chips(act):
        for other in range(n_chips - 1):
            pl.when(other < my_chip)(functools.partial(act, other))

    def share(c):
        mate_copy(c).wait()
        chip[:, inside(c), :] = total[:, inside(c), :] + mate[:, inside(c), :]
        later_chips(lambda other: chip_copy(other, c).start())

    for step in range(STEPS):
        last = step == STEPS - 1

        @pl.loop(0, chunks)
        def _(c):
            if step > 0:
                sent_chunk(step - 1, c)
            both("lon", lambda side: lon_copy(step, side, c, True).wait_recv())
            both("lat", lambda side: lat_copy(step, side, c, True).wait_recv())
            for side, edge in ((0, 0), (1, chunks - 1)):
                if sizes["lev"] > 1:
                    pl.when(jnp.logical_and(c == edge, has("lev", side)))(
                        functools.partial(take_lev, step, side)
                    )
            sums = update(step, c)
            if last:
                for p in range(J):
                    total[p, inside(c), :] = sums[p]
                mate_copy(c).start()
                pl.when(c > 0)(lambda: share(c - 1))
            else:
                send_chunk(step + 1, c)
                for side, edge in ((0, 0), (1, chunks - 1)):

                    def pass_on(side=side):
                        if step > 0:
                            lev_copy(step - 1, side).wait_send()
                        send_lev(step + 1, side)

                    if sizes["lev"] > 1:
                        pl.when(jnp.logical_and(c == edge, has("lev", side)))(pass_on)

    share(chunks - 1)
    before[...] = jnp.where(my_core == 1, mate[...], 0.0)

    def add(other):
        for c in range(chunks):
            chip_copy(0, c, other).wait_recv()
        before[...] += chip_in[other]

    earlier_chips(add)

    for step in (STEPS - 2, STEPS - 1):
        both("lev", lambda side: lev_copy(step, side).wait_send())
    for c in range(chunks):
        sent_chunk(STEPS - 1, c)
        later_chips(lambda other: chip_copy(other, c).wait_send())


def totals_kernel(scale, x, before, totals, end, sums, end_sem, sums_sem):
    J, I = x.shape[:2]

    def out(which, j):
        src, dst, sem = ((x, end, end_sem), (sums, totals, sums_sem))[which]
        return pltpu.make_async_copy(src.at[j], dst.at[j], sem.at[j])

    for j in range(J):
        out(0, j).start()

    @pl.loop(0, J)
    def _(j):
        def row(i, total):
            total = total + x[j, i]
            sums[j, i] = total * scale
            return total

        lax.fori_loop(0, I, row, before[j], unroll=4)
        out(1, j).start()

    for j in range(J):
        out(0, j).wait()
        out(1, j).wait()


def per_device(sizes, initial_state, scaled_diffusivity, scaled_forcing):
    J, I, K, M = initial_state.shape
    chunks = K // CHUNK
    n_lon = sizes["lon"]
    n_chips = n_lon // CORES
    f32 = jnp.float32
    vmem = lambda *shape: pltpu.VMEM(shape, f32)
    sem = lambda *shape: pltpu.SemaphoreType.DMA(shape)
    hbm = pl.BlockSpec(memory_space=pltpu.HBM)
    local = pl.BlockSpec(memory_space=pltpu.VMEM)
    end, before = pl.pallas_call(
        functools.partial(steps_kernel, sizes),
        out_shape=(vmem(J, I, K, M), vmem(J, K, M)),
        in_specs=[hbm] * 3,
        out_specs=(local, local),
        scratch_shapes=[
            vmem(J + 2, I + 2, K + 2 * PAD, M),
            vmem(J + 2, I + 2, K + 2 * PAD, M),
            vmem(J, I, K, M),
            vmem(J, I, K, M),
            vmem(2, 2, J, I, 1, M),
            vmem(2, 2, J, I, 1, M),
            vmem(J, K, M),
            vmem(J, K, M),
            vmem(J, K, M),
            vmem(n_chips, J, K, M),
            sem(2, 2, chunks),
            sem(2, 2, chunks),
            sem(2, 2, chunks),
            sem(2, 2, chunks),
            sem(2, 2),
            sem(2, 2),
            sem(3, J),
            sem(chunks),
            sem(chunks),
            sem(n_chips, chunks),
            sem(n_chips, chunks),
        ],
        compiler_params=pltpu.CompilerParams(
            collective_id=0, has_side_effects=True, vmem_limit_bytes=50 * 2**20
        ),
        name="steps",
    )(initial_state, scaled_diffusivity, scaled_forcing)

    return pl.pallas_call(
        functools.partial(totals_kernel, 1.0 / (I * n_lon)),
        out_shape=(jax.ShapeDtypeStruct((J, I, K, M), f32),) * 2,
        in_specs=[local, local],
        out_specs=(hbm, hbm),
        scratch_shapes=[vmem(J, I, K, M), sem(J), sem(J)],
        compiler_params=pltpu.CompilerParams(vmem_limit_bytes=20 * 2**20),
        name="totals",
    )(end, before)


def solution(mesh):
    spec = P("lat", "lon", "lev", None)
    return jax.shard_map(
        functools.partial(per_device, dict(mesh.shape)),
        mesh=mesh,
        in_specs=(spec,) * 3,
        out_specs=(spec,) * 2,
        check_vma=False,
    )
```

time: 170 us -> 135 us (0.79)
  Pallas kernels: 168 us -> 134 us
    pallas_call x1, Pallas kernels: 162 us -> 128 us  [per_device(): pl.pallas_call(functools.partial(steps_kernel, sizes), out_shape=(vmem(J,...]
where the time goes in v1:
time: 135 us
  Pallas kernels  134 us (99%)
    pallas_call x1, Pallas kernels, per_device(): pl.pallas_call(functools.partial(steps_kernel, sizes), out_shape=(vmem(J,...  128 us
    pallas_call x1, Pallas kernels, per_device(): pl.pallas_call(functools.partial(totals_kernel, 1.0 / (I * n_lon)), out_s...  5.96 us

profile of v1, /device:TPU:57, one launch (start us, length us, event | category | flops | bytes accessed | tf_op | source)
XLA Modules:
  0.0 134.6 jit_solution(2450108546658288049)
XLA Ops:
  0.6 128.0 %steps.1 = (f32[8,32,64,128]{3,2,1,0:T(8,128)S(1)}, f32[8,64,128]{2,1,0:T(8,128)S(1)}) custom-call(f32[8,32,64,128]{3,2,1,0:T(8,128)} %x.1, f32[8,32,64,128]{3,2,1,0:T(8,128)} %d.1, f32[8,32,64,128]{3,2,1,0:T(8,128)} %f.1), custom_call_target="tpu_custom_call" | custom-call | tf_op jit(solution)/shard_map/steps/pallas_call | solution.py:359
  128.7 6.0 %totals.1 = (f32[8,32,64,128]{3,2,1,0:T(8,128)}, f32[8,32,64,128]{3,2,1,0:T(8,128)}) custom-call(f32[8,32,64,128]{3,2,1,0:T(8,128)S(1)} %get-tuple-element.4.x, f32[8,64,128]{2,1,0:T(8,128)S(1)} %get-tuple-element.5.before), custom_call_target="tpu_custom_call" | custom-call | tf_op jit(solution)/shard_map/totals/pallas_call | solution.py:393

commit v2 on v1

--- a/solution.py
+++ b/solution.py
@@ -11,14 +11,17 @@
 PAD = 8
 CHUNK = 8
 CORES = 2
+EARLY = 2
+RELAYS = 3
 MESH = pl.DeviceIdType.MESH
 
 
 def steps_kernel(
     sizes, x, d, f, end, before, even, odd, coef, source,
-    lev_out, lev_in, total, mate, chip, chip_in,
+    lev_out, lev_in, total, mate, chip, chip_in, mine, theirs, edge, edge_in, relay,
     lat_send, lat_recv, lon_send, lon_recv, lev_send, lev_recv,
-    load_sem, mate_send, mate_recv, chip_send, chip_recv,
+    load_sem, mate_send, mate_recv, chip_send, chip_recv, half_sem, edge_send, edge_recv,
+    relay_send, relay_recv, pass_send, pass_recv,
 ):
     J, I, K, M = x.shape
     chunks = K // CHUNK
@@ -28,6 +31,7 @@
     n_chips = n_lon // CORES
     my_chip = me["lon"] // CORES
     my_core = me["lon"] % CORES
+    half = J // CORES
     rows = pl.ds(1, I)
     levels = pl.ds(PAD, K)
     planes = pl.ds(1, J)
@@ -94,24 +98,93 @@
             device_id_type=MESH,
         )
 
-    def lon_copy(step, side, c, arriving=False):
+    def lon_copy(step, side, c, arriving=False, count=J):
         slot = step % 2
         state = states[slot]
         row, target = (1, I + 1) if side == 0 else (I, 0)
         if arriving:
             target = 0 if side == 0 else I + 1
         if step == 0:
-            src = x.at[:, row - 1, inside(c)]
+            src = x.at[pl.ds(0, count), row - 1, inside(c)]
         else:
-            src = state.at[planes, row, padded(c)]
+            src = state.at[pl.ds(1, count), row, padded(c)]
         return pltpu.make_async_remote_copy(
             src_ref=src,
-            dst_ref=state.at[planes, target, padded(c)],
+            dst_ref=state.at[pl.ds(1, count), target, padded(c)],
             send_sem=lon_send.at[slot, side, c],
             recv_sem=lon_recv.at[slot, side if arriving else 1 - side, c],
             device_id=beside("lon", side),
             device_id_type=MESH,
         )
+
+    def to_relay(step, side, c):
+        row = 1 if side == 0 else I
+        if step == 0:
+            src = x.at[pl.ds(half, half), row - 1, inside(c)]
+        else:
+            src = states[step % 2].at[pl.ds(1 + half, half), row, padded(c)]
+        return pltpu.make_async_remote_copy(
+            src_ref=src,
+            dst_ref=relay.at[step, :, inside(c)],
+            send_sem=relay_send.at[step, c],
+            recv_sem=relay_recv.at[step, c],
+            device_id={"lon": jnp.int32(0 if side == 0 else n_lon - 1)},
+            device_id_type=MESH,
+        )
+
+    def from_relay(step, side, c):
+        target = I + 1 if side == 0 else 0
+        return pltpu.make_async_remote_copy(
+            src_ref=relay.at[step, :, inside(c)],
+            dst_ref=states[step % 2].at[pl.ds(1 + half, half), target, padded(c)],
+            send_sem=pass_send.at[step, c],
+            recv_sem=pass_recv.at[step, c],
+            device_id={"lon": jnp.int32(n_lon // 2 - 1 if side == 0 else n_lon // 2)},
+            device_id_type=MESH,
+        )
+
+    def lon_each(step, whole, split):
+        for side in (0, 1):
+            halved = me["lon"] == (n_lon // 2 if side == 0 else n_lon // 2 - 1)
+            if step < RELAYS:
+                pl.when(jnp.logical_and(has("lon", side), jnp.logical_not(halved)))(
+                    functools.partial(whole, side)
+                )
+                pl.when(halved)(functools.partial(split, side))
+            else:
+                pl.when(has("lon", side))(functools.partial(whole, side))
+
+    def start_lon(step, c):
+        def split(side):
+            to_relay(step, side, c).start()
+            lon_copy(step, side, c, count=half).start()
+
+        lon_each(step, lambda side: lon_copy(step, side, c).start(), split)
+
+    def sent_lon(step, c):
+        def split(side):
+            to_relay(step, side, c).wait_send()
+            lon_copy(step, side, c, count=half).wait_send()
+
+        lon_each(step, lambda side: lon_copy(step, side, c).wait_send(), split)
+
+    def arrived_lon(step, c):
+        def split(side):
+            from_relay(step, 1 - side, c).wait_recv()
+            lon_copy(step, side, c, True, half).wait_recv()
+
+        lon_each(step, lambda side: lon_copy(step, side, c, True).wait_recv(), split)
+
+    def relays(act):
+        for side in (0, 1):
+            pl.when(me["lon"] == (0 if side == 0 else n_lon - 1))(functools.partial(act, side))
+
+    def forward(step, c):
+        def act(side):
+            to_relay(step, side, c).wait_recv()
+            from_relay(step, side, c).start()
+
+        relays(act)
 
     def lev_copy(step, side, arriving=False):
         slot = step % 2
@@ -126,11 +199,11 @@
         )
 
     def send_chunk(step, c):
-        both("lon", lambda side: lon_copy(step, side, c).start())
+        start_lon(step, c)
         both("lat", lambda side: lat_copy(step, side, c).start())
 
     def sent_chunk(step, c):
-        both("lon", lambda side: lon_copy(step, side, c).wait_send())
+        sent_lon(step, c)
         both("lat", lambda side: lat_copy(step, side, c).wait_send())
 
     def send_lev(step, side):
@@ -152,9 +225,9 @@
         def _(p):
             state[p, 1 : I + 1, row : row + 1, :] = lev_in[step % 2, side, p - 1]
 
-    @pl.loop(0, chunks)
-    def _(c):
-        send_chunk(0, c)
+    pl.loop(0, EARLY)(lambda c: send_chunk(0, c))
+    pl.loop(0, chunks)(lambda c: forward(0, c))
+    pl.loop(EARLY, chunks)(lambda c: send_chunk(0, c))
 
     def clear(axis, side):
         for state in states:
@@ -188,7 +261,7 @@
         load(1, j).wait()
         load(2, j).wait()
 
-    def update(step, c):
+    def update(step, c, first, count):
         now, later = states[step % 2], states[(step + 1) % 2]
         last = step == STEPS - 1
         start = pl.multiple_of(PAD + c * CHUNK, CHUNK)
@@ -197,21 +270,22 @@
 
         def row(i, carry):
             past, mid, sums = carry
-            coming = tuple(now[p, i + 1, here, :] for p in range(1, J + 1))
-            column = (now[0, i, here, :],) + mid + (now[J + 1, i, here, :],)
+            coming = tuple(now[first + n, i + 1, here, :] for n in range(count))
+            column = (now[first - 1, i, here, :],) + mid + (now[first + count, i, here, :],)
             out = []
-            for p in range(1, J + 1):
+            for n in range(count):
+                p = first + n
                 spread = (
-                    (column[p - 1] + column[p + 1])
-                    + (past[p - 1] + coming[p - 1])
+                    (column[n] + column[n + 2])
+                    + (past[n] + coming[n])
                     + (
                         now[p, i, pl.ds(start - 1, CHUNK), :]
                         + now[p, i, pl.ds(start + 1, CHUNK), :]
                     )
-                    - 6.0 * column[p]
+                    - 6.0 * mid[n]
                 )
                 new = (
-                    column[p]
+                    mid[n]
                     + coef[p - 1, i - 1, inner, :] * spread
                     + source[p - 1, i - 1, inner, :]
                 )
@@ -230,13 +304,19 @@
             I + 1,
             row,
             (
-                tuple(now[p, 0, here, :] for p in range(1, J + 1)),
-                tuple(now[p, 1, here, :] for p in range(1, J + 1)),
-                (zero,) * J if last else (),
+                tuple(now[first + n, 0, here, :] for n in range(count)),
+                tuple(now[first + n, 1, here, :] for n in range(count)),
+                (zero,) * count if last else (),
             ),
-            unroll=2,
+            unroll=2 if count > 1 else 4,
         )
         return sums
+
+    my_half = pl.ds(half * my_core, half)
+    other_half = pl.ds(half * (1 - my_core), half)
+    inner_plane = 1 + me["lat"]
+    edge_plane = jnp.where(me["lat"] == 0, J, 1)
+    partner = {"lon": me["lon"] + 1 - 2 * my_core}
 
     def mate_copy(c):
         return pltpu.make_async_remote_copy(
@@ -244,7 +324,7 @@
             dst_ref=mate.at[:, inside(c)],
             send_sem=mate_send.at[c],
             recv_sem=mate_recv.at[c],
-            device_id={"lon": me["lon"] + 1 - 2 * my_core},
+            device_id=partner,
             device_id_type=MESH,
         )
 
@@ -259,6 +339,27 @@
             device_id_type=MESH,
         )
 
+    def half_copy():
+        return pltpu.make_async_remote_copy(
+            src_ref=mine,
+            dst_ref=theirs,
+            send_sem=half_sem.at[0],
+            recv_sem=half_sem.at[1],
+            device_id=partner,
+            device_id_type=MESH,
+        )
+
+    def edge_copy(target, arriving=None):
+        sender = me["lon"] if arriving is None else arriving
+        return pltpu.make_async_remote_copy(
+            src_ref=edge,
+            dst_ref=edge_in.at[sender],
+            send_sem=edge_send.at[target],
+            recv_sem=edge_recv.at[sender],
+            device_id={"lon": jnp.int32(target)},
+            device_id_type=MESH,
+        )
+
     def later_chips(act):
         for other in range(1, n_chips):
             pl.when(other > my_chip)(functools.partial(act, other))
@@ -267,58 +368,123 @@
         for other in range(n_chips - 1):
             pl.when(other < my_chip)(functools.partial(act, other))
 
+    def later_cores(act):
+        for other in range(1, n_lon):
+            pl.when(other > me["lon"])(functools.partial(act, other))
+
+    def earlier_cores(act):
+        for other in range(n_lon - 1):
+            pl.when(other < me["lon"])(functools.partial(act, other))
+
     def share(c):
         mate_copy(c).wait()
-        chip[:, inside(c), :] = total[:, inside(c), :] + mate[:, inside(c), :]
+        chip[:, inside(c), :] = total[my_half, inside(c), :] + mate[my_half, inside(c), :]
         later_chips(lambda other: chip_copy(other, c).start())
 
-    for step in range(STEPS):
-        last = step == STEPS - 1
+    def take_lon(step, c):
+        arrived_lon(step, c)
+        for side, end_chunk in ((0, 0), (1, chunks - 1)):
+            pl.when(jnp.logical_and(c == end_chunk, has("lev", side)))(
+                functools.partial(take_lev, step, side)
+            )
+
+    def send_lat(step, c):
+        both("lat", lambda side: lat_copy(step, side, c).start())
+
+    def take_lat(step, c):
+        both("lat", lambda side: lat_copy(step, side, c, True).wait_recv())
+
+    for step in range(STEPS - 1):
+        if 0 < step < RELAYS:
+            forward(step, chunks - 1)
 
         @pl.loop(0, chunks)
         def _(c):
             if step > 0:
                 sent_chunk(step - 1, c)
-            both("lon", lambda side: lon_copy(step, side, c, True).wait_recv())
-            both("lat", lambda side: lat_copy(step, side, c, True).wait_recv())
-            for side, edge in ((0, 0), (1, chunks - 1)):
-                if sizes["lev"] > 1:
-                    pl.when(jnp.logical_and(c == edge, has("lev", side)))(
-                        functools.partial(take_lev, step, side)
-                    )
-            sums = update(step, c)
-            if last:
-                for p in range(J):
-                    total[p, inside(c), :] = sums[p]
-                mate_copy(c).start()
-                pl.when(c > 0)(lambda: share(c - 1))
+            take_lon(step, c)
+            take_lat(step, c)
+            update(step, c, 1, J)
+            if step + 1 < RELAYS:
+                pl.when(c > 0)(lambda: forward(step + 1, c - 1))
+            if step < STEPS - 2:
+                send_chunk(step + 1, c)
             else:
-                send_chunk(step + 1, c)
-                for side, edge in ((0, 0), (1, chunks - 1)):
-
-                    def pass_on(side=side):
-                        if step > 0:
-                            lev_copy(step - 1, side).wait_send()
-                        send_lev(step + 1, side)
-
-                    if sizes["lev"] > 1:
-                        pl.when(jnp.logical_and(c == edge, has("lev", side)))(pass_on)
-
-    share(chunks - 1)
-    before[...] = jnp.where(my_core == 1, mate[...], 0.0)
-
-    def add(other):
+                start_lon(step + 1, c)
+                pl.when(c < EARLY)(lambda: send_lat(step + 1, c))
+            for side, end_chunk in ((0, 0), (1, chunks - 1)):
+
+                def pass_on(side=side):
+                    if step > 0:
+                        lev_copy(step - 1, side).wait_send()
+                    send_lev(step + 1, side)
+
+                pl.when(jnp.logical_and(c == end_chunk, has("lev", side)))(pass_on)
+
+    last = STEPS - 1
+    for c in range(EARLY, chunks):
+        send_lat(last, c)
+
+    @pl.loop(0, chunks)
+    def _(c):
+        sent_chunk(last - 1, c)
+        take_lon(last, c)
+        sums = update(last, c, inner_plane, J - 1)
+        for n in range(J - 1):
+            total[inner_plane - 1 + n, inside(c), :] = sums[n]
+
+    def edge_step(c):
+        take_lat(last, c)
+        return update(last, c, edge_plane, 1)[0]
+
+    tail = chunks - 1
+    total[edge_plane - 1, inside(tail), :] = jnp.zeros((CHUNK, M), jnp.float32)
+    mate_copy(tail).start()
+
+    @pl.loop(0, tail)
+    def _(c):
+        total[edge_plane - 1, inside(c), :] = edge_step(c)
+        mate_copy(c).start()
+        pl.when(c > 0)(lambda: share(c - 1))
+
+    share(tail)
+    share(tail - 1)
+    edge[...] = edge_step(tail)
+    later_cores(lambda other: edge_copy(other).start())
+
+    mine[...] = jnp.zeros(mine.shape, jnp.float32)
+
+    def add_chip(other):
         for c in range(chunks):
             chip_copy(0, c, other).wait_recv()
-        before[...] += chip_in[other]
-
-    earlier_chips(add)
+        mine[...] += chip_in[other]
+
+    earlier_chips(add_chip)
+    half_copy().start()
+    before[my_half] = mine[...]
+    half_copy().wait()
+    before[other_half] = theirs[...]
+
+    @pl.when(my_core == 1)
+    def _():
+        before[...] += mate[...]
+
+    def add_edge(other):
+        edge_copy(0, other).wait_recv()
+        before[edge_plane - 1, inside(tail), :] += edge_in[other]
+
+    earlier_cores(add_edge)
 
     for step in (STEPS - 2, STEPS - 1):
         both("lev", lambda side: lev_copy(step, side).wait_send())
     for c in range(chunks):
         sent_chunk(STEPS - 1, c)
         later_chips(lambda other: chip_copy(other, c).wait_send())
+    later_cores(lambda other: edge_copy(other).wait_send())
+    for step in range(RELAYS):
+        pl.loop(0, chunks)(
+            lambda c: relays(lambda side: from_relay(step, side, c).wait_send())
+        )
 
 
 def totals_kernel(scale, x, before, totals, end, sums, end_sem, sums_sem):
@@ -351,6 +517,7 @@
     chunks = K // CHUNK
     n_lon = sizes["lon"]
     n_chips = n_lon // CORES
+    half = J // CORES
     f32 = jnp.float32
     vmem = lambda *shape: pltpu.VMEM(shape, f32)
     sem = lambda *shape: pltpu.SemaphoreType.DMA(shape)
@@ -370,8 +537,13 @@
             vmem(2, 2, J, I, 1, M),
             vmem(J, K, M),
             vmem(J, K, M),
-            vmem(J, K, M),
-            vmem(n_chips, J, K, M),
+            vmem(half, K, M),
+            vmem(n_chips, half, K, M),
+            vmem(half, K, M),
+            vmem(half, K, M),
+            vmem(CHUNK, M),
+            vmem(n_lon, CHUNK, M),
+            vmem(RELAYS, half, K, M),
             sem(2, 2, chunks),
             sem(2, 2, chunks),
             sem(2, 2, chunks),
@@ -383,6 +555,13 @@
             sem(chunks),
             sem(n_chips, chunks),
             sem(n_chips, chunks),
+            sem(2),
+            sem(n_lon),
+            sem(n_lon),
+            sem(RELAYS, chunks),
+            sem(RELAYS, chunks),
+            sem(RELAYS, chunks),
+            sem(RELAYS, chunks),
         ],
         compiler_params=pltpu.CompilerParams(
             collective_id=0, has_side_effects=True, vmem_limit_bytes=50 * 2**20

time: 135 us -> 130 us (0.963)
  Pallas kernels: 134 us -> 129 us
    pallas_call x1, Pallas kernels: 128 us -> 123 us  [per_device(): pl.pallas_call(functools.partial(steps_kernel, sizes), out_shape=(vmem(J,...]
where the time goes in v2:
time: 130 us
  Pallas kernels  129 us (99%)
    pallas_call x1, Pallas kernels, per_device(): pl.pallas_call(functools.partial(steps_kernel, sizes), out_shape=(vmem(J,...  123 us
    pallas_call x1, Pallas kernels, per_device(): pl.pallas_call(functools.partial(totals_kernel, 1.0 / (I * n_lon)), out_s...  5.96 us

profile of v2, /device:TPU:57, one launch (start us, length us, event | category | flops | bytes accessed | tf_op | source)
XLA Modules:
  0.0 129.9 jit_solution(9072657573902150070)
XLA Ops:
  0.6 123.3 %steps.1 = (f32[8,32,64,128]{3,2,1,0:T(8,128)S(1)}, f32[8,64,128]{2,1,0:T(8,128)S(1)}) custom-call(f32[8,32,64,128]{3,2,1,0:T(8,128)} %x.1, f32[8,32,64,128]{3,2,1,0:T(8,128)} %d.1, f32[8,32,64,128]{3,2,1,0:T(8,128)} %f.1), custom_call_target="tpu_custom_call" | custom-call | tf_op jit(solution)/shard_map/steps/pallas_call | solution.py:526
  123.9 6.0 %totals.1 = (f32[8,32,64,128]{3,2,1,0:T(8,128)}, f32[8,32,64,128]{3,2,1,0:T(8,128)}) custom-call(f32[8,32,64,128]{3,2,1,0:T(8,128)S(1)} %get-tuple-element.4.x, f32[8,64,128]{2,1,0:T(8,128)S(1)} %get-tuple-element.5.before), custom_call_target="tpu_custom_call" | custom-call | tf_op jit(solution)/shard_map/totals/pallas_call | solution.py:572

commit v3 on v2

--- a/solution.py
+++ b/solution.py
@@ -12,7 +12,7 @@
 CHUNK = 8
 CORES = 2
 EARLY = 2
-RELAYS = 3
+AHEAD = 4
 MESH = pl.DeviceIdType.MESH
 
 
@@ -55,10 +55,6 @@
         )[which]
         return pltpu.make_async_copy(src, dst, load_sem.at[which, j])
 
-    for which in range(3):
-        for j in range(J):
-            load(which, j).start()
-
     barrier = pltpu.get_barrier_semaphore()
     count = jnp.int32(n_lon - 1)
 
@@ -71,6 +67,10 @@
             count = count + has(axis, 0).astype(jnp.int32) + has(axis, 1).astype(jnp.int32)
     for other in range(n_lon):
         pl.when(other != me["lon"])(lambda other=other: greet({"lon": jnp.int32(other)}))
+    for which in range(3):
+        for j in range(J):
+            load(which, j).start()
+
     pl.semaphore_wait(barrier, count)
 
     def inside(c):
@@ -143,10 +143,13 @@
             device_id_type=MESH,
         )
 
-    def lon_each(step, whole, split):
+    def relay_sides(step):
+        return (0, 1) if step < STEPS - 1 else (1,)
+
+    def lon_each(step, whole, split, arriving=False):
         for side in (0, 1):
             halved = me["lon"] == (n_lon // 2 if side == 0 else n_lon // 2 - 1)
-            if step < RELAYS:
+            if (1 - side if arriving else side) in relay_sides(step):
                 pl.when(jnp.logical_and(has("lon", side), jnp.logical_not(halved)))(
                     functools.partial(whole, side)
                 )
@@ -173,10 +176,10 @@
             from_relay(step, 1 - side, c).wait_recv()
             lon_copy(step, side, c, True, half).wait_recv()
 
-        lon_each(step, lambda side: lon_copy(step, side, c, True).wait_recv(), split)
-
-    def relays(act):
-        for side in (0, 1):
+        lon_each(step, lambda side: lon_copy(step, side, c, True).wait_recv(), split, True)
+
+    def relays(step, act):
+        for side in relay_sides(step):
             pl.when(me["lon"] == (0 if side == 0 else n_lon - 1))(functools.partial(act, side))
 
     def forward(step, c):
@@ -184,7 +187,7 @@
             to_relay(step, side, c).wait_recv()
             from_relay(step, side, c).start()
 
-        relays(act)
+        relays(step, act)
 
     def lev_copy(step, side, arriving=False):
         slot = step % 2
@@ -395,7 +398,7 @@
         both("lat", lambda side: lat_copy(step, side, c, True).wait_recv())
 
     for step in range(STEPS - 1):
-        if 0 < step < RELAYS:
+        if step > 0:
             forward(step, chunks - 1)
 
         @pl.loop(0, chunks)
@@ -405,7 +408,7 @@
             take_lon(step, c)
             take_lat(step, c)
             update(step, c, 1, J)
-            if step + 1 < RELAYS:
+            if step + 1 < STEPS - 1:
                 pl.when(c > 0)(lambda: forward(step + 1, c - 1))
             if step < STEPS - 2:
                 send_chunk(step + 1, c)
@@ -422,7 +425,10 @@
                 pl.when(jnp.logical_and(c == end_chunk, has("lev", side)))(pass_on)
 
     last = STEPS - 1
-    for c in range(EARLY, chunks):
+    for c in range(EARLY, AHEAD):
+        send_lat(last, c)
+    pl.loop(0, chunks)(lambda c: forward(last, c))
+    for c in range(AHEAD, chunks):
         send_lat(last, c)
 
     @pl.loop(0, chunks)
@@ -481,9 +487,9 @@
         sent_chunk(STEPS - 1, c)
         later_chips(lambda other: chip_copy(other, c).wait_send())
     later_cores(lambda other: edge_copy(other).wait_send())
-    for step in range(RELAYS):
+    for step in range(STEPS):
         pl.loop(0, chunks)(
-            lambda c: relays(lambda side: from_relay(step, side, c).wait_send())
+            lambda c: relays(step, lambda side: from_relay(step, side, c).wait_send())
         )
 
 
@@ -543,7 +549,7 @@
             vmem(half, K, M),
             vmem(CHUNK, M),
             vmem(n_lon, CHUNK, M),
-            vmem(RELAYS, half, K, M),
+            vmem(STEPS, half, K, M),
             sem(2, 2, chunks),
             sem(2, 2, chunks),
             sem(2, 2, chunks),
@@ -558,10 +564,10 @@
             sem(2),
             sem(n_lon),
             sem(n_lon),
-            sem(RELAYS, chunks),
-            sem(RELAYS, chunks),
-            sem(RELAYS, chunks),
-            sem(RELAYS, chunks),
+            sem(STEPS, chunks),
+            sem(STEPS, chunks),
+            sem(STEPS, chunks),
+            sem(STEPS, chunks),
         ],
         compiler_params=pltpu.CompilerParams(
             collective_id=0, has_side_effects=True, vmem_limit_bytes=50 * 2**20

time: 130 us -> 129 us (level)
  no operation moved by 1% of the time
where the time goes in v3:
time: 129 us
  Pallas kernels  128 us (99%)
    pallas_call x1, Pallas kernels, per_device(): pl.pallas_call(functools.partial(steps_kernel, sizes), out_shape=(vmem(J,...  122 us
    pallas_call x1, Pallas kernels, per_device(): pl.pallas_call(functools.partial(totals_kernel, 1.0 / (I * n_lon)), out_s...  5.96 us

profile of v3, /device:TPU:57, one launch (start us, length us, event | category | flops | bytes accessed | tf_op | source)
XLA Modules:
  0.0 128.9 jit_solution(7702927736699440374)
XLA Ops:
  0.6 122.3 %steps.1 = (f32[8,32,64,128]{3,2,1,0:T(8,128)S(1)}, f32[8,64,128]{2,1,0:T(8,128)S(1)}) custom-call(f32[8,32,64,128]{3,2,1,0:T(8,128)} %x.1, f32[8,32,64,128]{3,2,1,0:T(8,128)} %d.1, f32[8,32,64,128]{3,2,1,0:T(8,128)} %f.1), custom_call_target="tpu_custom_call" | custom-call | tf_op jit(solution)/shard_map/steps/pallas_call | solution.py:532
  122.9 6.0 %totals.1 = (f32[8,32,64,128]{3,2,1,0:T(8,128)}, f32[8,32,64,128]{3,2,1,0:T(8,128)}) custom-call(f32[8,32,64,128]{3,2,1,0:T(8,128)S(1)} %get-tuple-element.4.x, f32[8,64,128]{2,1,0:T(8,128)S(1)} %get-tuple-element.5.before), custom_call_target="tpu_custom_call" | custom-call | tf_op jit(solution)/shard_map/totals/pallas_call | solution.py:578

commit v4 on v3

--- a/solution.py
+++ b/solution.py
@@ -13,6 +13,8 @@
 CORES = 2
 EARLY = 2
 AHEAD = 4
+FIRST = 4
+ROUNDS = 4
 MESH = pl.DeviceIdType.MESH
 
 
@@ -21,7 +23,7 @@
     lev_out, lev_in, total, mate, chip, chip_in, mine, theirs, edge, edge_in, relay,
     lat_send, lat_recv, lon_send, lon_recv, lev_send, lev_recv,
     load_sem, mate_send, mate_recv, chip_send, chip_recv, half_sem, edge_send, edge_recv,
-    relay_send, relay_recv, pass_send, pass_recv,
+    relay_send, relay_recv, pass_send, pass_recv, rounds,
 ):
     J, I, K, M = x.shape
     chunks = K // CHUNK
@@ -56,22 +58,42 @@
         return pltpu.make_async_copy(src, dst, load_sem.at[which, j])
 
     barrier = pltpu.get_barrier_semaphore()
-    count = jnp.int32(n_lon - 1)
-
-    def greet(target):
-        pl.semaphore_signal(barrier, inc=1, device_id=target, device_id_type=MESH)
-
-    for axis in ("lat", "lev"):
-        both(axis, lambda side, axis=axis: greet(beside(axis, side)))
-        if sizes[axis] > 1:
-            count = count + has(axis, 0).astype(jnp.int32) + has(axis, 1).astype(jnp.int32)
-    for other in range(n_lon):
-        pl.when(other != me["lon"])(lambda other=other: greet({"lon": jnp.int32(other)}))
-    for which in range(3):
-        for j in range(J):
-            load(which, j).start()
-
-    pl.semaphore_wait(barrier, count)
+    lev_half, lon_half = sizes["lev"] // 2, n_lon // 2
+    across, deep = me["lon"] // CORES % 2, me["lon"] // lon_half
+    ring, lap = me["lev"] % lev_half, me["lev"] // lev_half
+    side_x = 2 * across + me["lat"]
+    side_z = 2 * lap + deep
+    spot = lambda axis, index: {axis: index}
+    near = (
+        (jnp.bool_(True), spot("lat", 1 - me["lat"])),
+        (jnp.bool_(True), spot("lon", me["lon"] + 1 - 2 * my_core)),
+        (jnp.bool_(True), spot("lon", me["lon"] + lon_half - 2 * lon_half * deep)),
+        (ring > 0, spot("lev", me["lev"] - 1)),
+        (ring < lev_half - 1, spot("lev", me["lev"] + 1)),
+        (
+            jnp.logical_or(side_x == 1, side_x == 2),
+            {"lat": 1 - me["lat"], "lon": me["lon"] + CORES - 2 * CORES * across},
+        ),
+        (
+            jnp.logical_or(side_z == 1, side_z == 2),
+            {
+                "lon": me["lon"] + lon_half - 2 * lon_half * deep,
+                "lev": me["lev"] + lev_half - 2 * lev_half * lap,
+            },
+        ),
+    )
+    peers = sum(there.astype(jnp.int32) for there, _ in near)
+
+    def meet(semaphore):
+        for there, target in near:
+            pl.when(there)(
+                lambda target=target: pl.semaphore_signal(
+                    semaphore, inc=1, device_id=target, device_id_type=MESH
+                )
+            )
+        pl.semaphore_wait(semaphore, peers)
+
+    meet(barrier)
 
     def inside(c):
         return pl.ds(pl.multiple_of(c * CHUNK, CHUNK), CHUNK)
@@ -228,9 +250,18 @@
         def _(p):
             state[p, 1 : I + 1, row : row + 1, :] = lev_in[step % 2, side, p - 1]
 
-    pl.loop(0, EARLY)(lambda c: send_chunk(0, c))
+    for c in range(FIRST):
+        both("lat", lambda side: lat_copy(0, side, c).start())
+    for which in range(3):
+        for j in range(J):
+            load(which, j).start()
+
+    for n in range(ROUNDS):
+        meet(rounds.at[n])
+    for c in range(FIRST):
+        start_lon(0, c)
     pl.loop(0, chunks)(lambda c: forward(0, c))
-    pl.loop(EARLY, chunks)(lambda c: send_chunk(0, c))
+    pl.loop(FIRST, chunks)(lambda c: send_chunk(0, c))
 
     def clear(axis, side):
         for state in states:
@@ -568,6 +599,7 @@
             sem(STEPS, chunks),
             sem(STEPS, chunks),
             sem(STEPS, chunks),
+            pltpu.SemaphoreType.REGULAR((ROUNDS,)),
         ],
         compiler_params=pltpu.CompilerParams(
             collective_id=0, has_side_effects=True, vmem_limit_bytes=50 * 2**20

time: 129 us -> 128 us (level)
    pallas_call x1, Pallas kernels: 122 us -> 121 us  [per_device(): pl.pallas_call(functools.partial(steps_kernel, sizes), out_shape=(vmem(J,...]
where the time goes in v4:
time: 128 us; the launch traced here: 127 us
  Pallas kernels  127 us (99%)
    pallas_call x1, Pallas kernels, per_device(): pl.pallas_call(functools.partial(steps_kernel, sizes), out_shape=(vmem(J,...  121 us
    pallas_call x1, Pallas kernels, per_device(): pl.pallas_call(functools.partial(totals_kernel, 1.0 / (I * n_lon)), out_s...  5.96 us

profile of v4, /device:TPU:57, one launch (start us, length us, event | category | flops | bytes accessed | tf_op | source)
XLA Modules:
  0.0 127.5 jit_solution(13890074157456538185)
XLA Ops:
  0.6 120.9 %steps.1 = (f32[8,32,64,128]{3,2,1,0:T(8,128)S(1)}, f32[8,64,128]{2,1,0:T(8,128)S(1)}) custom-call(f32[8,32,64,128]{3,2,1,0:T(8,128)} %x.1, f32[8,32,64,128]{3,2,1,0:T(8,128)} %d.1, f32[8,32,64,128]{3,2,1,0:T(8,128)} %f.1), custom_call_target="tpu_custom_call" | custom-call | tf_op jit(solution)/shard_map/steps/pallas_call | solution.py:563
  121.5 6.0 %totals.1 = (f32[8,32,64,128]{3,2,1,0:T(8,128)}, f32[8,32,64,128]{3,2,1,0:T(8,128)}) custom-call(f32[8,32,64,128]{3,2,1,0:T(8,128)S(1)} %get-tuple-element.4.x, f32[8,64,128]{2,1,0:T(8,128)S(1)} %get-tuple-element.5.before), custom_call_target="tpu_custom_call" | custom-call | tf_op jit(solution)/shard_map/totals/pallas_call | solution.py:610

commit v5 on v4

--- a/solution.py
+++ b/solution.py
@@ -256,12 +256,13 @@
         for j in range(J):
             load(which, j).start()
 
-    for n in range(ROUNDS):
+    for n in range(ROUNDS - 1):
         meet(rounds.at[n])
     for c in range(FIRST):
         start_lon(0, c)
     pl.loop(0, chunks)(lambda c: forward(0, c))
     pl.loop(FIRST, chunks)(lambda c: send_chunk(0, c))
+    meet(rounds.at[ROUNDS - 1])
 
     def clear(axis, side):
         for state in states:

time: 128 us -> 128 us (level)
  no operation moved by 1% of the time
where the time goes in v5:
time: 128 us; the launch traced here: 127 us
  Pallas kernels  127 us (99%)
    pallas_call x1, Pallas kernels, per_device(): pl.pallas_call(functools.partial(steps_kernel, sizes), out_shape=(vmem(J,...  121 us
    pallas_call x1, Pallas kernels, per_device(): pl.pallas_call(functools.partial(totals_kernel, 1.0 / (I * n_lon)), out_s...  5.96 us

profile of v5, /device:TPU:57, one launch (start us, length us, event | category | flops | bytes accessed | tf_op | source)
XLA Modules:
  0.0 127.5 jit_solution(17967593467105455739)
XLA Ops:
  0.6 120.9 %steps.1 = (f32[8,32,64,128]{3,2,1,0:T(8,128)S(1)}, f32[8,64,128]{2,1,0:T(8,128)S(1)}) custom-call(f32[8,32,64,128]{3,2,1,0:T(8,128)} %x.1, f32[8,32,64,128]{3,2,1,0:T(8,128)} %d.1, f32[8,32,64,128]{3,2,1,0:T(8,128)} %f.1), custom_call_target="tpu_custom_call" | custom-call | tf_op jit(solution)/shard_map/steps/pallas_call | solution.py:564
  121.5 6.0 %totals.1 = (f32[8,32,64,128]{3,2,1,0:T(8,128)}, f32[8,32,64,128]{3,2,1,0:T(8,128)}) custom-call(f32[8,32,64,128]{3,2,1,0:T(8,128)S(1)} %get-tuple-element.4.x, f32[8,64,128]{2,1,0:T(8,128)S(1)} %get-tuple-element.5.before), custom_call_target="tpu_custom_call" | custom-call | tf_op jit(solution)/shard_map/totals/pallas_call | solution.py:611
